TPU v7x, 512 devices: a whole 4x4x16 slice. The times are simulated.
512 devices in a mesh: grp: 4 (over x), dom: 128 (over z, y, core).
Axes of the slice: x: 4, y: 4, z: 16, core: 2. Of those that a mesh axis runs over, the one named last changes fastest.
Arguments:
- node_state: float32 [65536, 6, 128], P(('grp', 'dom')), may hold values from -6 to 6
- node_dest: int32 [65536], P(('grp', 'dom')), may hold values from 0 to 127, as said below
- seg_nodes: float32 [6, 262144], P(None, ('grp', 'dom')), may hold values from -6 to 6
- seg_conn: int32 [3, 524288], P(None, ('grp', 'dom')), may hold values from 0 to 511
- pair_seg: int32 [512, 4, 32], P(('grp', 'dom')), may hold values from 0 to 7
- pair_slot: int32 [512, 4, 32], P(('grp', 'dom')), may hold values from 0 to 255, as said below
Outputs:
- node_force: float32 [65536, 3, 128], P(('grp', 'dom'))
Inputs may be any that keep to these rules, and one draw needn't show every extreme that they name: `node_dest`: at most 2 blocks of one device name the same contact domain; in every grp row one contact domain receives exactly 2 blocks from every device of that row; every device sends at least one block to the contact domain of its own dom index. `pair_slot`: every entry names a slot d * 2 + k that holds a block: device (r, d) sends more than k blocks to the contact domain.
All inputs are finite; a program needn't handle non-finite values.
Results may differ from a plain program's by a relative error of at most 0.00023.
Values sent between devices are 32-bit elements; how exact they have to be, the bound alone decides.
No kernel may reach another device: no remote copies, remote signals or barrier semaphores. Data moves between devices by JAX's collectives and lax.ppermute only.
A program may use at most 64 MiB of HBM per device.

v0:
```python
import jax
import jax.numpy as jnp
from jax import lax
from jax.sharding import Mesh
from jax.sharding import PartitionSpec as P

SEG_BLK = 128
DOM = ("dom_0", "dom_1", "dom_2")
GRP_DOM = ("grp", "dom_0", "dom_1", "dom_2")
time_step = 0.5
stiffness = 0.5
radius_sq = 0.5


def in_blocks(shard, dim, devices):
    dims = shard.shape
    blocks = shard.reshape(*dims[:dim], devices, dims[dim] // devices, *dims[dim + 1 :])
    return jnp.moveaxis(blocks, dim, 0)


def in_order(blocks, dim):
    blocks = jnp.moveaxis(blocks, 0, dim)
    dims = blocks.shape
    return blocks.reshape(*dims[:dim], dims[dim] * dims[dim + 1], *dims[dim + 2 :])


def moved_by_axis(blocks, axes, turns):
    dims = [lax.axis_size(a) for a in axes]
    blocks = blocks.reshape(*dims, *blocks.shape[1:])
    for k in turns:
        blocks = lax.all_to_all(blocks, axes[k], split_axis=k, concat_axis=k, tiled=True)
    return blocks.reshape(-1, *blocks.shape[len(axes) :])


def two_step_exchange(shard, groups, turns, split_dim, concat_dim):
    devices = lax.axis_size(groups[0]) * lax.axis_size(groups[1])
    blocks = in_blocks(shard, split_dim, devices)
    return in_order(moved_by_axis(blocks, groups, turns), concat_dim)


def seg_geometry(corners):
    corner_a = corners[:, 0]
    corner_b = corners[:, 1]
    corner_c = corners[:, 2]
    edge_one = corner_b[0:3] - corner_a[0:3]
    edge_two = corner_c[0:3] - corner_a[0:3]
    normal = 0.5 * jnp.stack(
        [
            edge_one[1] * edge_two[2] - edge_one[2] * edge_two[1],
            edge_one[2] * edge_two[0] - edge_one[0] * edge_two[2],
            edge_one[0] * edge_two[1] - edge_one[1] * edge_two[0],
        ]
    )
    centre = (corner_a[0:3] + corner_b[0:3] + corner_c[0:3]) / 3.0
    motion = (corner_a[3:6] + corner_b[3:6] + corner_c[3:6]) / 3.0
    return jnp.concatenate([normal, centre, motion], axis=0)


def tile_force(node_rows, geometry):
    clearance = jnp.zeros((geometry.shape[1], node_rows.shape[1]), jnp.float32)
    distance = jnp.zeros((geometry.shape[1], node_rows.shape[1]), jnp.float32)
    for axis_id in range(3):
        offset = node_rows[axis_id][None, :] - geometry[3 + axis_id][:, None]
        drift = node_rows[3 + axis_id][None, :] - geometry[6 + axis_id][:, None]
        clearance = clearance + geometry[axis_id][:, None] * (offset + time_step * drift)
        distance = distance + offset * offset
    pressure = stiffness * jnp.exp(-distance / radius_sq) * jnp.maximum(-clearance, 0.0)
    return jnp.dot(
        geometry[0:3], pressure, precision=lax.Precision.HIGHEST, preferred_element_type=jnp.float32
    )


def place_rows(slot_ids, values, slot_total):
    onehot = (slot_ids[None, :] == jnp.arange(slot_total, dtype=jnp.int32)[:, None]).astype(
        jnp.float32
    )
    flattened = values.reshape(values.shape[0], -1)
    placed = jnp.dot(
        onehot, flattened, precision=lax.Precision.HIGHEST, preferred_element_type=jnp.float32
    )
    return placed.reshape((slot_total,) + values.shape[1:])


def shards(node_state, node_dest, seg_nodes, seg_conn, pair_seg, pair_slot):
    dom_count = lax.axis_size(DOM)
    grp_count = lax.axis_size("grp")
    block_count = node_state.shape[0]
    capacity = max(2, 2 * block_count // dom_count)
    slot_count = dom_count * capacity
    order_ids = jnp.arange(block_count, dtype=jnp.int32)
    earlier = order_ids[None, :] < order_ids[:, None]
    same_dom = node_dest[:, None] == node_dest[None, :]
    slot_rank = jnp.sum((same_dom & earlier).astype(jnp.int32), axis=1)
    target_slot = node_dest * capacity + slot_rank
    outgoing = place_rows(target_slot, node_state, slot_count)
    received = two_step_exchange(outgoing, (("dom_0", "dom_1"), "dom_2"), (1, 0), 0, 0)
    corners = jnp.take(seg_nodes, seg_conn, axis=1)
    geometry = seg_geometry(corners)
    seg_blocks = geometry.shape[1] // SEG_BLK
    geo_blocks = jnp.transpose(geometry.reshape(9, seg_blocks, SEG_BLK), (1, 0, 2))
    seg_table = pair_seg[0]
    slot_table = pair_slot[0]
    geo_all = lax.all_gather(geo_blocks, "grp", axis=0, tiled=True)
    seg_in, slot_in = (
        lax.all_to_all(seg_table, "grp", split_axis=0, concat_axis=0, tiled=True),
        lax.all_to_all(slot_table, "grp", split_axis=0, concat_axis=0, tiled=True),
    )
    owner_base = (jnp.arange(grp_count, dtype=jnp.int32) * seg_blocks)[:, None]
    seg_ids = (seg_in + owner_base).reshape(-1)
    slot_ids = slot_in.reshape(-1)
    forces = jax.vmap(tile_force)(
        jnp.take(received, slot_ids, axis=0), jnp.take(geo_all, seg_ids, axis=0)
    )
    own_forces = place_rows(slot_ids, forces, slot_count)
    returned = lax.all_to_all(own_forces, DOM, split_axis=0, concat_axis=0, tiled=True)
    return jnp.take(returned, target_slot, axis=0)


def solution(mesh):
    split = Mesh(
        mesh.devices.reshape(mesh.shape["grp"], 16, 4, 2), ("grp", "dom_0", "dom_1", "dom_2")
    )
    placed = (
        P(GRP_DOM, None, None),
        P(GRP_DOM),
        P(None, GRP_DOM),
        P(None, GRP_DOM),
        P(GRP_DOM, None, None),
        P(GRP_DOM, None, None),
    )
    return jax.shard_map(
        shards, mesh=split, in_specs=placed, out_specs=P(GRP_DOM, None, None), check_vma=False
    )
```

profile of v0, /device:TPU:33, one launch (start us, length us, event | category | flops | bytes accessed | tf_op | source)
XLA Modules:
  0.0 168.8 jit_solution(1052670801400604042)
XLA Ops:
  0.0 0.9 convert_reduce_fusion
  0.9 0.7 compare_and_fusion.3
  1.6 1.2 copy.65
  3.3 4.7 %all_to_all.39 = f32[64,2,2,6,128]{4,0,3,2,1:T(8,128)S(1)} all-to-all(f32[64,2,2,6,128]{4,0,3,2,1:T(8,128)S(1)} %fusion.34), channel_id=1, replica_groups=mesh['grp'=4,'dom_0'=16,'dom_1'=4,'dom_2'=2] {'dom_2'}, dimensions={1} | all-to-all | bytes 1572864 | tf_op jit(solution)/shard_map/all_to_all | solution.py:31
  8.0 4.0 %all-to-all-start.1 = ((s32[4,1,32]{2,1,0:T(1,128)}), s32[4,1,32]{2,1,0:T(1,128)S(1)}, u32[]{:S(2)}, u32[]{:S(2)}) async-start(s32[4,1,32]{2,1,0:T(1,128)} %bitcast.4), calls=%async_computation.1 | async-start | bytes 4096 | tf_op jit(solution)/shard_map/all_to_all | solution.py:105
  12.0 4.0 %all-to-all-done.1 = s32[4,1,32]{2,1,0:T(1,128)S(1)} async-done(((s32[4,1,32]{2,1,0:T(1,128)}), s32[4,1,32]{2,1,0:T(1,128)S(1)}, u32[]{:S(2)}, u32[]{:S(2)}) %all-to-all-start.1) | async-done | bytes 544 | tf_op jit(solution)/shard_map/all_to_all | solution.py:105
  16.0 3.2 %all-to-all-start = ((s32[4,1,32]{2,1,0:T(1,128)}), s32[4,1,32]{2,1,0:T(1,128)S(1)}, u32[]{:S(2)}, u32[]{:S(2)}) async-start(s32[4,1,32]{2,1,0:T(1,128)} %bitcast.1), calls=%async_computation | async-start | bytes 4096 | tf_op jit(solution)/shard_map/all_to_all | solution.py:106
  19.3 1.5 copy.66
  20.8 2.5 %all-to-all-done = s32[4,1,32]{2,1,0:T(1,128)S(1)} async-done(((s32[4,1,32]{2,1,0:T(1,128)}), s32[4,1,32]{2,1,0:T(1,128)S(1)}, u32[]{:S(2)}, u32[]{:S(2)}) %all-to-all-start) | async-done | bytes 544 | tf_op jit(solution)/shard_map/all_to_all | solution.py:106
  23.3 17.8 %all-to-all-start.3 = ((f32[64,2,2,6,128]{4,2,3,1,0:T(2,128)}), f32[64,2,2,6,128]{4,2,3,1,0:T(2,128)S(1)}, u32[]{:S(2)}, u32[]{:S(2)}) async-start(f32[64,2,2,6,128]{4,2,3,1,0:T(2,128)} %copy.66), calls=%async_computation.3 | async-start | bytes 1572864 | tf_op jit(solution)/shard_map/all_to_all | solution.py:31
  41.5 8.1 %gather_fusion = f32[3072,6]{1,0:T(8,128)S(1)} fusion(f32[6,512]{0,1:T(8,128)S(1)} %copy.62, s32[3072]{0:T(1024)S(1)} %broadcast_clamp_fusion), kind=kCustom, calls=%fused_computation | custom fusion | bytes 159744 | tf_op jit(solution)/shard_map/jit(_take)/gather | solution.py:97
  50.3 9.9 %all_gather.3 = f32[32,9,128]{2,0,1:T(8,128)S(1)} all-gather(f32[8,9,128]{2,0,1:T(8,128)S(1)} %maximum_bitcast_fusion), channel_id=1, replica_groups=mesh['grp'=4,'dom_0'=16,'dom_1'=4,'dom_2'=2] {'grp'}, dimensions={0}, use_global_device_ids=true | all-gather | bytes 184320 | tf_op jit(solution)/shard_map/all_gather | solution.py:103
  60.3 0.5 broadcast.150
  60.8 0.7 reduce.10
  61.7 0.7 reduce.11
  62.4 0.8 gather_fusion.1
  63.9 16.5 %all-to-all-done.3 = f32[64,2,2,6,128]{4,2,3,1,0:T(2,128)S(1)} async-done(((f32[64,2,2,6,128]{4,2,3,1,0:T(2,128)}), f32[64,2,2,6,128]{4,2,3,1,0:T(2,128)S(1)}, u32[]{:S(2)}, u32[]{:S(2)}) %all-to-all-start.3) | async-done | bytes 786464 | tf_op jit(solution)/shard_map/all_to_all | solution.py:31
  81.1 0.8 gather_fusion.2
  82.4 37.2 %fusion.14 = f32[128,3,128]{2,1,0:T(4,128)S(1)} fusion(f32[128,128]{1,0:T(8,128)S(1)} %bitcast.77, f32[128,128]{1,0:T(8,128)S(1)} %bitcast.86, f32[128,128]{1,0:T(8,128)S(1)} %bitcast.78, f32[128,128]{1,0:T(8,128)S(1)} %bitcast.79, f32[128,128]{1,0:T(8,128)S(1)} %bitcast.87, f32[128,128]{1,0:T(8,128)S(1)} %bitcast.80, f32[128,128]{1,0:T(8,128)S(1)} %bitcast.81, ...), kind=kOutput, calls=%fused_computation.24 | convolution fusion | flops 134217728 | bytes 1441792 | tf_op jit(solution)/shard_map/vmap()/dot_general | solution.py:68
  120.1 1.1 copy.70
  121.2 12.2 %all-to-all-start.4 = ((f32[256,3,128]{2,1,0:T(4,128)}), f32[256,3,128]{2,1,0:T(4,128)S(1)}, u32[]{:S(2)}, u32[]{:S(2)}) async-start(f32[256,3,128]{2,1,0:T(4,128)} %copy.70), calls=%async_computation.4 | async-start | bytes 1048576 | tf_op jit(solution)/shard_map/all_to_all | solution.py:115
  133.5 33.7 %all-to-all-done.4 = f32[256,3,128]{2,1,0:T(4,128)S(1)} async-done(((f32[256,3,128]{2,1,0:T(4,128)}), f32[256,3,128]{2,1,0:T(4,128)S(1)}, u32[]{:S(2)}, u32[]{:S(2)}) %all-to-all-start.4) | async-done | bytes 393248 | tf_op jit(solution)/shard_map/all_to_all | solution.py:115
  167.1 0.8 gather_fusion.3
  168.1 0.7 copy.71
  (44 shorter events, 4.5 us)
Async XLA Ops:
  2.7 9.2 %copy-start = (s32[3,1024]{1,0:T(4,128)S(1)}, s32[3,1024]{1,0:T(4,128)}, u32[]{:S(2)}) copy-start(s32[3,1024]{1,0:T(4,128)} %param.9) | copy-start | bytes 36868
  8.0 8.1 %all-to-all-start.1 = ((s32[4,1,32]{2,1,0:T(1,128)}), s32[4,1,32]{2,1,0:T(1,128)S(1)}, u32[]{:S(2)}, u32[]{:S(2)}) async-start(s32[4,1,32]{2,1,0:T(1,128)} %bitcast.4), calls=%async_computation.1 | async-start | bytes 4096 | tf_op jit(solution)/shard_map/all_to_all | solution.py:105
  16.0 7.3 %all-to-all-start = ((s32[4,1,32]{2,1,0:T(1,128)}), s32[4,1,32]{2,1,0:T(1,128)S(1)}, u32[]{:S(2)}, u32[]{:S(2)}) async-start(s32[4,1,32]{2,1,0:T(1,128)} %bitcast.1), calls=%async_computation | async-start | bytes 4096 | tf_op jit(solution)/shard_map/all_to_all | solution.py:106
  19.3 22.1 %copy-start.1 = (f32[6,512]{1,0:T(8,128)S(1)}, f32[6,512]{1,0:T(8,128)}, u32[]{:S(2)}) copy-start(f32[6,512]{1,0:T(8,128)} %param.8) | copy-start | bytes 36868
  23.3 57.1 %all-to-all-start.3 = ((f32[64,2,2,6,128]{4,2,3,1,0:T(2,128)}), f32[64,2,2,6,128]{4,2,3,1,0:T(2,128)S(1)}, u32[]{:S(2)}, u32[]{:S(2)}) async-start(f32[64,2,2,6,128]{4,2,3,1,0:T(2,128)} %copy.66), calls=%async_computation.3 | async-start | bytes 1572864 | tf_op jit(solution)/shard_map/all_to_all | solution.py:31
  121.2 46.0 %all-to-all-start.4 = ((f32[256,3,128]{2,1,0:T(4,128)}), f32[256,3,128]{2,1,0:T(4,128)S(1)}, u32[]{:S(2)}, u32[]{:S(2)}) async-start(f32[256,3,128]{2,1,0:T(4,128)} %copy.70), calls=%async_computation.4 | async-start | bytes 1048576 | tf_op jit(solution)/shard_map/all_to_all | solution.py:115
where the time goes:
time: 169 us
  waiting for transfers between devices  56.7 us (34%)
  matrix products  38.1 us (23%)
  starting transfers between devices  37.3 us (22%)
  local copies, waits for them, and re-layouts  18.2 us (11%)
  blocking collectives  14.5 us (9%)
  other arithmetic  3.67 us (2%)
    dot_general x1, matrix products, tile_force(): jnp.dot(geometry[0:3], pressure, precision=lax.Precision.HIGHEST, preferr...  37.2 us
    all_to_all x1, waiting for transfers between devices, shards(): lax.all_to_all(own_forces, DOM, split_axis=0, concat_axis=0, tiled=True)  33.7 us
    all_to_all x1, starting transfers between devices, moved_by_axis(): lax.all_to_all(blocks, axes[k], split_axis=k, concat_axis=k, tiled=True)  17.8 us
    all_to_all x1, waiting for transfers between devices, moved_by_axis(): lax.all_to_all(blocks, axes[k], split_axis=k, concat_axis=k, tiled=True)  16.5 us
    all_to_all x1, starting transfers between devices, shards(): lax.all_to_all(own_forces, DOM, split_axis=0, concat_axis=0, tiled=True)  12.2 us
    all_gather x1, blocking collectives, shards(): geo_all = lax.all_gather(geo_blocks, 'grp', axis=0, tiled=True)  9.87 us
    gather x2, local copies, waits for them, and re-layouts, shards(): corners = jnp.take(seg_nodes, seg_conn, axis=1)  8.59 us
    all_to_all x1, blocking collectives, moved_by_axis(): lax.all_to_all(blocks, axes[k], split_axis=k, concat_axis=k, tiled=True)  4.67 us
  transfers between devices with their start and end apart: 4, of which 4 were waited for; matrix products, arithmetic and copies ran while one was open for 8% of the time, Pallas kernels for 0%

commit v1 on v0

--- a/solution.py
+++ b/solution.py
@@ -3,6 +3,7 @@
 from jax import lax
 from jax.sharding import Mesh
 from jax.sharding import PartitionSpec as P
+from jax.lax import axis_index, axis_size, ppermute
 
 SEG_BLK = 128
 DOM = ("dom_0", "dom_1", "dom_2")
@@ -10,6 +11,28 @@
 time_step = 0.5
 stiffness = 0.5
 radius_sq = 0.5
+
+
+def slabs_part(x_in, chip_axis):
+    out_arr = axis_size(chip_axis)
+    reply = axis_index(chip_axis)
+    tmp, local_next = (out_arr, reply)
+    inter = list(x_in.shape)
+    field_out = x_in.shape[0] // tmp
+    inter[0] = field_out
+    q_next = inter[0]
+    inter[0] = q_next * tmp
+    state_now = jnp.zeros(inter, x_in.dtype)
+    for t in range(tmp):
+        block_now = lax.dynamic_slice_in_dim(x_in, (local_next ^ t) * field_out, field_out, axis=0)
+        if t:
+            block_now = ppermute(
+                block_now, axis_name=chip_axis, perm=[(num, num ^ t) for num in range(tmp)]
+            )
+        state_now = lax.dynamic_update_slice_in_dim(
+            state_now, block_now, (local_next ^ t) * q_next, axis=0
+        )
+    return state_now
 
 
 def in_blocks(shard, dim, devices):
@@ -102,7 +125,7 @@
     slot_table = pair_slot[0]
     geo_all = lax.all_gather(geo_blocks, "grp", axis=0, tiled=True)
     seg_in, slot_in = (
-        lax.all_to_all(seg_table, "grp", split_axis=0, concat_axis=0, tiled=True),
+        slabs_part(seg_table, "grp"),
         lax.all_to_all(slot_table, "grp", split_axis=0, concat_axis=0, tiled=True),
     )
     owner_base = (jnp.arange(grp_count, dtype=jnp.int32) * seg_blocks)[:, None]

time: 169 us -> 183 us (1.083)
  the two profiles are of different devices: /device:TPU:33 before, /device:TPU:39 now
where the time goes in v1:
time: 183 us; the launch traced here: 182 us
  waiting for transfers between devices  62.9 us (34%)
  starting transfers between devices  41.1 us (22%)
  matrix products  38 us (21%)
  local copies, waits for them, and re-layouts  20.7 us (11%)
  blocking collectives  16.1 us (9%)
  other arithmetic  3.13 us (2%)
    dot_general x1, matrix products, tile_force(): jnp.dot(geometry[0:3], pressure, precision=lax.Precision.HIGHEST, preferr...  37.1 us
    all_to_all x1, waiting for transfers between devices, shards(): lax.all_to_all(own_forces, DOM, split_axis=0, concat_axis=0, tiled=True)  33.7 us
    all_to_all x1, waiting for transfers between devices, moved_by_axis(): lax.all_to_all(blocks, axes[k], split_axis=k, concat_axis=k, tiled=True)  29.2 us
    all_to_all x1, starting transfers between devices, moved_by_axis(): lax.all_to_all(blocks, axes[k], split_axis=k, concat_axis=k, tiled=True)  17.8 us
    all_gather x1, blocking collectives, shards(): geo_all = lax.all_gather(geo_blocks, 'grp', axis=0, tiled=True)  10 us
    ppermute x3, starting transfers between devices, slabs_part(): ppermute(block_now, axis_name=chip_axis, perm=[(num, num ^ t) for num in...  9.57 us
    all_to_all x1, starting transfers between devices, shards(): lax.all_to_all(own_forces, DOM, split_axis=0, concat_axis=0, tiled=True)  9.48 us
    gather x2, local copies, waits for them, and re-layouts, shards(): corners = jnp.take(seg_nodes, seg_conn, axis=1)  8.59 us
  transfers between devices with their start and end apart: 6, of which 2 were waited for; matrix products, arithmetic and copies ran while one was open for 10% of the time, Pallas kernels for 0%

profile of v1, /device:TPU:39, one launch (start us, length us, event | category | flops | bytes accessed | tf_op | source)
XLA Modules:
  0.0 182.2 jit_solution(963501544666832464)
XLA Ops:
  0.0 4.2 %all-to-all-start = ((s32[4,1,32]{2,1,0:T(1,128)}), s32[4,1,32]{2,1,0:T(1,128)S(1)}, u32[]{:S(2)}, u32[]{:S(2)}) async-start(s32[4,1,32]{2,1,0:T(1,128)} %bitcast.99), calls=%async_computation | async-start | bytes 4096 | tf_op jit(solution)/shard_map/all_to_all | solution.py:129
  4.2 0.8 fusion.52
  5.0 1.9 %collective-permute-start.2 = (s32[1,32]{1,0:T(1,128)S(1)}, s32[1,32]{1,0:T(1,128)S(1)}, u32[]{:S(2)}, u32[]{:S(2)}) collective-permute-start(s32[1,32]{1,0:T(1,128)S(1)} %get-tuple-element.29), channel_id=1, source_target_pairs={{0,384},{128,256},{256,128},{384,0},{1,385},{129,257},{257,129},{3... | collective-permute-start | bytes 392 | tf_op jit(solution)/shard_map/ppermute | solution.py:29
  7.0 2.8 %collective-permute-start = (s32[1,32]{1,0:T(1,128)S(1)}, s32[1,32]{1,0:T(1,128)S(1)}, u32[]{:S(2)}, u32[]{:S(2)}) collective-permute-start(s32[1,32]{1,0:T(1,128)S(1)} %get-tuple-element.30), channel_id=1, source_target_pairs={{0,128},{128,0},{256,384},{384,256},{1,129},{129,1},{257,385},{385... | collective-permute-start | bytes 392 | tf_op jit(solution)/shard_map/ppermute | solution.py:29
  9.7 4.9 %collective-permute-start.1 = (s32[1,32]{1,0:T(1,128)S(1)}, s32[1,32]{1,0:T(1,128)S(1)}, u32[]{:S(2)}, u32[]{:S(2)}) collective-permute-start(s32[1,32]{1,0:T(1,128)S(1)} %get-tuple-element.32), channel_id=1, source_target_pairs={{0,256},{128,384},{256,0},{384,128},{1,257},{129,385},{257,1},{385... | collective-permute-start | bytes 392 | tf_op jit(solution)/shard_map/ppermute | solution.py:29
  14.7 0.9 convert_reduce_fusion
  15.6 0.7 compare_select_fusion
  16.3 0.9 copy.59
  17.2 1.2 copy.62
  18.4 8.1 %gather_fusion = f32[3072,6]{1,0:T(8,128)S(1)} fusion(f32[6,512]{0,1:T(8,128)S(1)} %copy.59, s32[3072]{0:T(1024)S(1)} %broadcast_clamp_fusion), kind=kCustom, calls=%fused_computation | custom fusion | bytes 159744 | tf_op jit(solution)/shard_map/jit(_take)/gather | solution.py:120
  28.8 6.1 %all_to_all.24 = f32[64,2,2,6,128]{4,0,3,2,1:T(8,128)S(1)} all-to-all(f32[64,2,2,6,128]{4,0,3,2,1:T(8,128)S(1)} %fusion.34), channel_id=1, replica_groups=mesh['grp'=4,'dom_0'=16,'dom_1'=4,'dom_2'=2] {'dom_2'}, dimensions={1} | all-to-all | bytes 1572864 | tf_op jit(solution)/shard_map/all_to_all | solution.py:54
  34.8 1.5 copy.63
  36.4 17.8 %all-to-all-start.2 = ((f32[64,2,2,6,128]{4,2,3,1,0:T(2,128)}), f32[64,2,2,6,128]{4,2,3,1,0:T(2,128)S(1)}, u32[]{:S(2)}, u32[]{:S(2)}) async-start(f32[64,2,2,6,128]{4,2,3,1,0:T(2,128)} %copy.63), calls=%async_computation.2 | async-start | bytes 1572864 | tf_op jit(solution)/shard_map/all_to_all | solution.py:54
  54.4 10.0 %all_gather.3 = f32[32,9,128]{2,0,1:T(8,128)S(1)} all-gather(f32[8,9,128]{2,0,1:T(8,128)S(1)} %maximum_bitcast_fusion), channel_id=1, replica_groups=mesh['grp'=4,'dom_0'=16,'dom_1'=4,'dom_2'=2] {'grp'}, dimensions={0}, use_global_device_ids=true | all-gather | bytes 184320 | tf_op jit(solution)/shard_map/all_gather | solution.py:126
  64.9 0.8 gather_fusion.1
  65.9 1.0 fusion.58
  67.0 29.2 %all-to-all-done.2 = f32[64,2,2,6,128]{4,2,3,1,0:T(2,128)S(1)} async-done(((f32[64,2,2,6,128]{4,2,3,1,0:T(2,128)}), f32[64,2,2,6,128]{4,2,3,1,0:T(2,128)S(1)}, u32[]{:S(2)}, u32[]{:S(2)}) %all-to-all-start.2) | async-done | bytes 786464 | tf_op jit(solution)/shard_map/all_to_all | solution.py:54
  97.0 0.8 gather_fusion.2
  98.7 37.1 %fusion.14 = f32[128,3,128]{2,1,0:T(4,128)S(1)} fusion(f32[128,128]{1,0:T(8,128)S(1)} %bitcast.81, f32[128,128]{1,0:T(8,128)S(1)} %bitcast.90, f32[128,128]{1,0:T(8,128)S(1)} %bitcast.82, f32[128,128]{1,0:T(8,128)S(1)} %bitcast.83, f32[128,128]{1,0:T(8,128)S(1)} %bitcast.91, f32[128,128]{1,0:T(8,128)S(1)} %bitcast.84, f32[128,128]{1,0:T(8,128)S(1)} %bitcast.85, ...), kind=kOutput, calls=%fused_computation.24 | convolution fusion | flops 134217728 | bytes 1441792 | tf_op jit(solution)/shard_map/vmap()/dot_general | solution.py:91
  136.3 1.1 copy.67
  137.4 9.5 %all-to-all-start.3 = ((f32[256,3,128]{2,1,0:T(4,128)}), f32[256,3,128]{2,1,0:T(4,128)S(1)}, u32[]{:S(2)}, u32[]{:S(2)}) async-start(f32[256,3,128]{2,1,0:T(4,128)} %copy.67), calls=%async_computation.3 | async-start | bytes 1048576 | tf_op jit(solution)/shard_map/all_to_all | solution.py:138
  146.9 33.7 %all-to-all-done.3 = f32[256,3,128]{2,1,0:T(4,128)S(1)} async-done(((f32[256,3,128]{2,1,0:T(4,128)}), f32[256,3,128]{2,1,0:T(4,128)S(1)}, u32[]{:S(2)}, u32[]{:S(2)}) %all-to-all-start.3) | async-done | bytes 393248 | tf_op jit(solution)/shard_map/all_to_all | solution.py:138
  180.6 0.8 gather_fusion.3
  181.5 0.7 copy.68
  (56 shorter events, 5.5 us)
Async XLA Ops:
  0.0 27.0 %all-to-all-start = ((s32[4,1,32]{2,1,0:T(1,128)}), s32[4,1,32]{2,1,0:T(1,128)S(1)}, u32[]{:S(2)}, u32[]{:S(2)}) async-start(s32[4,1,32]{2,1,0:T(1,128)} %bitcast.99), calls=%async_computation | async-start | bytes 4096 | tf_op jit(solution)/shard_map/all_to_all | solution.py:129
  5.0 59.6 %collective-permute-start.2 = (s32[1,32]{1,0:T(1,128)S(1)}, s32[1,32]{1,0:T(1,128)S(1)}, u32[]{:S(2)}, u32[]{:S(2)}) collective-permute-start(s32[1,32]{1,0:T(1,128)S(1)} %get-tuple-element.29), channel_id=1, source_target_pairs={{0,384},{128,256},{256,128},{384,0},{1,385},{129,257},{257,129},{3... | collective-permute-start | bytes 392 | tf_op jit(solution)/shard_map/ppermute | solution.py:29
  7.0 57.6 %collective-permute-start = (s32[1,32]{1,0:T(1,128)S(1)}, s32[1,32]{1,0:T(1,128)S(1)}, u32[]{:S(2)}, u32[]{:S(2)}) collective-permute-start(s32[1,32]{1,0:T(1,128)S(1)} %get-tuple-element.30), channel_id=1, source_target_pairs={{0,128},{128,0},{256,384},{384,256},{1,129},{129,1},{257,385},{385... | collective-permute-start | bytes 392 | tf_op jit(solution)/shard_map/ppermute | solution.py:29
  9.7 54.9 %collective-permute-start.1 = (s32[1,32]{1,0:T(1,128)S(1)}, s32[1,32]{1,0:T(1,128)S(1)}, u32[]{:S(2)}, u32[]{:S(2)}) collective-permute-start(s32[1,32]{1,0:T(1,128)S(1)} %get-tuple-element.32), channel_id=1, source_target_pairs={{0,256},{128,384},{256,0},{384,128},{1,257},{129,385},{257,1},{385... | collective-permute-start | bytes 392 | tf_op jit(solution)/shard_map/ppermute | solution.py:29
  17.2 11.1 %copy-start.4 = (s32[128]{0:T(128)S(1)}, s32[128]{0:T(128)}, u32[]{:S(2)}) copy-start(s32[128]{0:T(128)} %param.7) | copy-start | bytes 1540
  34.8 19.4 %copy-start.3 = (s32[3,1024]{1,0:T(4,128)S(1)}, s32[3,1024]{1,0:T(4,128)}, u32[]{:S(2)}) copy-start(s32[3,1024]{1,0:T(4,128)} %param.9) | copy-start | bytes 36868
  36.4 59.9 %all-to-all-start.2 = ((f32[64,2,2,6,128]{4,2,3,1,0:T(2,128)}), f32[64,2,2,6,128]{4,2,3,1,0:T(2,128)S(1)}, u32[]{:S(2)}, u32[]{:S(2)}) async-start(f32[64,2,2,6,128]{4,2,3,1,0:T(2,128)} %copy.63), calls=%async_computation.2 | async-start | bytes 1572864 | tf_op jit(solution)/shard_map/all_to_all | solution.py:54
  97.8 0.8 copy-start
  97.8 0.9 copy-start.1
  97.8 0.9 copy-start.2
  137.4 43.2 %all-to-all-start.3 = ((f32[256,3,128]{2,1,0:T(4,128)}), f32[256,3,128]{2,1,0:T(4,128)S(1)}, u32[]{:S(2)}, u32[]{:S(2)}) async-start(f32[256,3,128]{2,1,0:T(4,128)} %copy.67), calls=%async_computation.3 | async-start | bytes 1048576 | tf_op jit(solution)/shard_map/all_to_all | solution.py:138
